TPU v7x, 256 devices: a whole 4x4x8 slice. The times are simulated.
256 devices in a mesh: north: 8 (over x, core), east: 32 (over z, y).
Axes of the slice: x: 4, y: 4, z: 8, core: 2. Of those that a mesh axis runs over, the one named last changes fastest.
Arguments:
- left_factor: bfloat16 [8192, 8192], P('north', 'east'), may hold values from -6 to 6
- right_factor: bfloat16 [8192, 16384], P('north', 'east'), may hold values from -0.0625 to 0.0625
Outputs:
- updated: float32 [8192, 16384], P('north', 'east')
All inputs are finite; a program needn't handle non-finite values.
Results may differ from a plain program's by a relative error of at most 0.0003.
Values may be sent and summed in bfloat16 or wider, within the bound.
A program may use at most 128 MiB of HBM per device.

v0:
```python
import functools

import jax
import jax.numpy as jnp
from jax import lax
from jax.experimental import pallas as pl
from jax.experimental.pallas import tpu as pltpu
from jax.sharding import PartitionSpec as P

MESH = pl.DeviceIdType.MESH
LANES = 128
GROUPS = 4
TOP = 32768.0
TAIL = 16
LINK_RATE = 46.6e3
CORE_RATE = 600e3
LINK_LATENCY = 2.0
CORE_LATENCY = 1.0
WINDOW = 2.5
MULTIPLY = 0.5
FINISH = 0.6
UNITS = [(0, 0), (1, 1), (3, 0), (2, 0), (2, 1), (1, 0), (3, 1), (0, 1)]
USES = {
    ("dir", 0): (1, 1), ("dir", 1): (3, 0),
    ("two", 0): (2, 0), ("two", 1): (2, 1),
    ("acc", 0): (1, 0), ("acc", 1): (3, 1),
}
KINDS = ("two", "dir", "acc")


class Item:
    def __init__(self, key, deps, rank, emit, link=None, size=0, takes=0.0):
        self.key, self.deps, self.rank, self.emit = key, deps, rank, emit
        self.link, self.size, self.takes = link, size, takes


def plan(items):
    ready, free, order = {}, {}, []
    left = list(items)
    now = 0.0
    while left:
        best = None
        for item in left:
            if any(d not in ready for d in item.deps):
                continue
            at = max([ready[d] for d in item.deps], default=0.0)
            if item.link:
                at = max(at, free.get(item.link, 0.0) - WINDOW)
            at = max(at, now)
            trial = (at, 0 if item.link else 1, item.rank)
            if best is None or trial < best[0]:
                best = (trial, item)
        (at, _, _), item = best
        now = at
        if item.link:
            near = item.link == "core"
            begin = max(now, free.get(item.link, 0.0))
            free[item.link] = begin + item.size / (CORE_RATE if near else LINK_RATE)
            ready[item.key] = free[item.link] + (CORE_LATENCY if near else LINK_LATENCY)
            now += 0.03
        else:
            now += item.takes
            ready[item.key] = now
        order.append(item)
        left.remove(item)
    return order, ready


def kernel(
    xs, ys, zs, a_hbm, b_hbm, out, left, right, relay, code_out, code_in,
    sums_own, sums_in, load, sent, came, s_sent, s_came,
):
    rows, depth = a_hbm.shape
    columns = b_hbm.shape[1]
    n = ys * zs
    half = columns // 2
    group = rows // GROUPS
    chunk = group // 2

    me_north, me = lax.axis_index("north"), lax.axis_index("east")
    x, core = lax.div(me_north, 2), lax.rem(me_north, 2)
    z, y = lax.div(me, ys), lax.rem(me, ys)

    def turn(v, by, size):
        return lax.rem(v + (by + size), size)

    def x_at(by):
        return 2 * turn(x, by, xs) + core

    def y_at(by):
        return z * ys + turn(y, by, ys)

    def z_at(by):
        return turn(z, by, zs) * ys + y

    partner = (2 * x + 1 - core, me)
    toward = {
        "x0": (x_at(1), me), "x1": (x_at(-1), me),
        "y0": (me_north, y_at(1)), "y1": (me_north, y_at(-1)),
        "z0": (me_north, z_at(1)), "z1": (me_north, z_at(-1)),
        "core": partner,
    }

    def slab(north):
        return pl.ds(pl.multiple_of(north * depth, depth), depth)

    def cols(h):
        return pl.ds(h * half, half)

    own_left = left.at[:, slab(z)]
    load_a = pltpu.make_async_copy(a_hbm, own_left, load.at[0])
    load_b = pltpu.make_async_copy(b_hbm.at[slab(y)], right.at[0, slab(me_north)], load.at[1])
    load_a.start()
    load_b.start()

    barrier = pltpu.get_barrier_semaphore()
    for device in toward.values():
        pl.semaphore_signal(barrier, inc=1, device_id=device, device_id_type=MESH)
    pl.semaphore_wait(barrier, len(toward))

    items, copies, waits = [], {}, {("load", 0): load_a.wait, ("load", 1): load_b.wait}
    ready_at_start = [("load", 0), ("load", 1)]

    def send(key, deps, rank, link, source, target):
        i = len(copies)
        copy = pltpu.make_async_remote_copy(
            src_ref=source, dst_ref=target, send_sem=sent.at[i], recv_sem=came.at[i],
            device_id=toward[link], device_id_type=MESH,
        )
        copies[key] = copy
        waits[key] = copy.wait_recv
        size = 2 * source.shape[0] * source.shape[1]
        items.append(Item(key, deps, rank, copy.start, link, size))

    arrived = {p: [] for p in range(GROUPS)}
    for p in range(GROUPS):
        for s in range(2):
            here = pl.ds(p * group + s * chunk, chunk)
            for d in range(2):
                hops = zs // 2 - (s + d) % 2
                for h in range(hops):
                    block = left.at[here, slab(turn(z, h if d else -h, zs))]
                    key = ("a", p, s, d, h)
                    send(
                        key, [("a", p, s, d, h - 1)] if h else [], (p, h, s), f"z{d}",
                        block if h else a_hbm.at[here], block,
                    )
                    arrived[p].append(key)

    place = {u: i for i, u in enumerate(UNITS)}
    base = {}
    for d, j in ((0, 3), (1, 1)):
        block = b_hbm.at[slab(turn(y, -1 if d else 1, ys))]
        for h in range(2):
            base[j, h] = [("by", j, h)]
            send(
                ("by", j, h), [], (0, place[j, h]), f"y{d}",
                block.at[:, cols(h)], right.at[j, slab(me_north), cols(h)],
            )
    far = b_hbm.at[slab(turn(y, 2, ys))]
    for h in range(2):
        base[0, h], base[2, h] = [], [("by", 2, h)]
        send(("far", h), [], (0, place[2, h]), f"y{h}", far.at[:, cols(h)], relay.at[h])
        send(
            ("by", 2, h), [("far", h)], (0, place[2, h]), f"y{h}",
            relay.at[h], right.at[2, slab(me_north), cols(h)],
        )
    have = {}
    for u in UNITS:
        j, h = u
        rank = (0, place[u])
        mine = right.at[j, slab(me_north), cols(h)]
        source = mine if j else b_hbm.at[slab(y), cols(h)]
        landed = list(base[u]) if j else [("load", 1)]
        for d in range(2):
            send(("bx", u, d, 1), base[u], rank, f"x{d}", source, mine)
            landed.append(("bx", u, d, 1))
        passed = right.at[j, slab(x_at(1 if h else -1)), cols(h)]
        send(("bx", u, h, 2), [("bx", u, h, 1)], rank, f"x{h}", passed, passed)
        landed.append(("bx", u, h, 2))
        for t in range(xs):
            block = right.at[j, slab(x_at(-t)), cols(h)] if t else source
            target = right.at[j, slab(x_at(-t)), cols(h)]
            deps = [base[u], [("bx", u, 0, 1)], [("bx", u, h, 2)], [("bx", u, 1, 1)]][t]
            send(("bd", u, t), deps, rank, "core", block, target)
            landed.append(("bd", u, t))
        have[u] = landed

    def multiply(p, u):
        j, h = u
        return jnp.dot(
            left[p * group:(p + 1) * group, :], right[j, :, h * half:(h + 1) * half],
            preferred_element_type=jnp.float32,
        )

    def decode(p, k):
        coded = code_in[p, k, :group, :].astype(jnp.float32)
        scale = code_in[p, k, group:group + 1, :].astype(jnp.float32) * (1.0 / TOP)
        size = lax.rsqrt(lax.rsqrt(jnp.maximum(jnp.abs(coded), 1e-37)))
        size = size * lax.rsqrt(size)
        return jnp.where(coded < 0, -size, size) * scale

    def encode(p, k, value):
        most = jnp.maximum(jnp.max(jnp.abs(value), axis=0, keepdims=True), 1e-30)
        scale = most.astype(jnp.bfloat16)
        power = value * (TOP / scale.astype(jnp.float32))
        power = power * power
        power = power * power
        power = power * power
        code_out[p, k, :group, :] = jnp.where(value < 0, -power, power).astype(jnp.bfloat16)
        code_out[p, k, group:, :] = jnp.broadcast_to(scale, (TAIL, half))

    def slot(kind, d):
        return 2 * KINDS.index(kind) + d

    def part(p, kind, d):
        def run():
            value = multiply(p, USES[kind, d])
            if kind == "acc":
                value = value + decode(p, slot("two", d))
            encode(p, slot(kind, d), value)
        return run

    def own(p, h):
        def run():
            out[p * group:(p + 1) * group, h * half:(h + 1) * half] = multiply(p, (0, h))
        return run

    def finish(p):
        def run():
            here = slice(p * group, (p + 1) * group)
            narrow = None
            for h in range(2):
                value = out[here, h * half:(h + 1) * half]
                value = value + decode(p, slot("dir", 1 - h)) + decode(p, slot("acc", h))
                out[here, h * half:(h + 1) * half] = value
                value = value * value
                for k in range(0, half, LANES):
                    term = value[:, k:k + LANES]
                    narrow = term if narrow is None else narrow + term
            sums_own[:, here] = jnp.sum(narrow.T, axis=0, keepdims=True)
        return run

    for p in range(GROUPS):
        rows_in = arrived[p] + [("load", 0)]
        for k, kind in enumerate(KINDS):
            for d in range(2):
                deps = rows_in + have[USES[kind, d]]
                if kind == "acc":
                    deps = deps + [("c", p, "two", d)]
                items.append(Item(("k", p, kind, d), deps, (p, k, d), part(p, kind, d), takes=MULTIPLY))
                i = slot(kind, d)
                send(
                    ("c", p, kind, d), [("k", p, kind, d)], (1, p, k), f"y{d}",
                    code_out.at[p, i], code_in.at[p, i],
                )
        for h in range(2):
            items.append(Item(("own", p, h), rows_in + have[0, h], (p + GROUPS, 0, h), own(p, h), takes=MULTIPLY))
        deps = [("own", p, 0), ("own", p, 1)]
        deps += [("c", p, kind, d) for kind in ("dir", "acc") for d in range(2)]
        items.append(Item(("fin", p), deps, (p, 9, 0), finish(p), takes=FINISH))

    shares = ((0, (GROUPS - 1) * group), ((GROUPS - 1) * group, group))
    s_copies = [
        [
            pltpu.make_async_remote_copy(
                src_ref=sums_own.at[:, pl.ds(*share)], dst_ref=sums_in.at[k - 1, :, pl.ds(*share)],
                send_sem=s_sent.at[i, k - 1], recv_sem=s_came.at[i, k - 1],
                device_id=(me_north, lax.rem(me + k, n)), device_id_type=MESH,
            )
            for k in range(1, n)
        ]
        for i, share in enumerate(shares)
    ]

    def tell(i):
        def run():
            for copy in s_copies[i]:
                copy.start()
        return run

    items.append(Item(("s", 0), [("fin", p) for p in range(GROUPS - 1)], (GROUPS, 0), tell(0), takes=0.5))
    items.append(Item(("s", 1), [("fin", GROUPS - 1)], (GROUPS, 1), tell(1), takes=0.5))

    for key in ready_at_start:
        items.insert(0, Item(key, [], (-1,), lambda: None))
    order, _ = plan(items)
    waited = set()
    for item in order:
        for key in item.deps:
            if key in waits and key not in waited:
                waits[key]()
                waited.add(key)
        item.emit()
    for key in waits:
        if key not in waited:
            waits[key]()

    for group_copies in s_copies:
        for copy in group_copies:
            copy.wait_recv()
    total = sums_own[...]
    for k in range(n - 1):
        total = total + sums_in[k]
    scale = lax.rsqrt(total / (columns * n) + 1e-06)
    piece = 256
    for begin in range(0, rows, piece):
        gain = jnp.broadcast_to(scale[:, begin:begin + piece], (LANES, piece)).T
        for k in range(0, columns, LANES):
            out[pl.ds(begin, piece), k:k + LANES] *= gain
    for copy in copies.values():
        copy.wait_send()
    for group_copies in s_copies:
        for copy in group_copies:
            copy.wait_send()


def shards(xs, ys, zs, left, right):
    rows, depth = left.shape
    columns = right.shape[1]
    half = columns // 2
    group = rows // GROUPS
    peers = ys * zs - 1
    count = 14 * 2 * GROUPS // 2 * (zs // 8) + 8 + 8 * 7 + 6 * GROUPS
    dma = pltpu.SemaphoreType.DMA
    count = GROUPS * 2 * (zs - 1) + 8 + 7 * len(UNITS) + 6 * GROUPS
    return pl.pallas_call(
        functools.partial(kernel, xs, ys, zs),
        out_shape=jax.ShapeDtypeStruct((rows, columns), jnp.float32),
        in_specs=[pl.BlockSpec(memory_space=pl.ANY)] * 2,
        out_specs=pl.BlockSpec(memory_space=pltpu.VMEM),
        scratch_shapes=[
            pltpu.VMEM((rows, depth * zs), left.dtype),
            pltpu.VMEM((ys, depth * 2 * xs, columns), right.dtype),
            pltpu.VMEM((2, depth, half), right.dtype),
            pltpu.VMEM((GROUPS, 6, group + TAIL, half), jnp.bfloat16),
            pltpu.VMEM((GROUPS, 6, group + TAIL, half), jnp.bfloat16),
            pltpu.VMEM((1, rows), jnp.float32),
            pltpu.VMEM((peers, 1, rows), jnp.float32),
            dma((2,)),
            dma((count,)),
            dma((count,)),
            dma((2, peers)),
            dma((2, peers)),
        ],
        compiler_params=pltpu.CompilerParams(
            collective_id=0, has_side_effects=True, vmem_limit_bytes=56 << 20
        ),
    )(left, right)


def solution(mesh):
    xs = mesh.shape["north"] // 2
    ys = xs
    zs = mesh.shape["east"] // ys
    placed = (P("north", "east"), P("north", "east"))
    return jax.shard_map(
        functools.partial(shards, xs, ys, zs),
        mesh=mesh, in_specs=placed, out_specs=P("north", "east"), check_vma=False,
    )
```

profile of v0, /device:TPU:1, one launch (start us, length us, event | category | flops | bytes accessed | tf_op | source)
XLA Modules:
  0.0 93.1 jit_solution(10994350036674278438)
XLA Ops:
  0.0 90.0 %shard_map.28 = f32[1024,512]{1,0:T(8,128)} custom-call(bf16[1024,256]{1,0:T(8,128)(2,1)} %a_hbm.1, bf16[1024,512]{1,0:T(8,128)(2,1)} %b_hbm.1), custom_call_target="tpu_custom_call" | custom-call | tf_op jit(solution)/shard_map/pallas_call | solution.py:327
  90.0 3.1 %copy.4 = f32[1024,512]{1,0:T(8,128)} copy(f32[1024,512]{1,0:T(8,128)} %shard_map.28) | data formatting | bytes 4194304
where the time goes:
time: 93.2 us; the launch traced here: 93.1 us
  Pallas kernels  90 us (97%)
  local copies, waits for them, and re-layouts  3.08 us (3%)
    pallas_call x1, Pallas kernels, shards(): pl.pallas_call(functools.partial(kernel, xs, ys, zs), out_shape=jax.Shape...  90 us
    unnamed x1, local copies, waits for them, and re-layouts  3.08 us

commit v1 on v0

v1 whole, which is shorter than its diff:
```python
import functools

import jax
import jax.numpy as jnp
from jax import lax
from jax.experimental import pallas as pl
from jax.experimental.pallas import tpu as pltpu
from jax.sharding import PartitionSpec as P

MESH = pl.DeviceIdType.MESH
LANES = 128
GROUPS = (192, 192, 192, 192, 128, 128)
LATE = 4
EARLY = 2
TOP = 32768.0
TAIL = 8
HEAD = 16
LINK_RATE = 46.6e3
CORE_RATE = 600e3
LINK_LATENCY = 2.8
CORE_LATENCY = 1.0
FAR_SOURCE = 0.5
WINDOW = 2.5
SLACK = 0.0
PACE = 3
MULTIPLY = 0.7 / 256
CODE = 0.13 / 256
FINISH = 0.53 / 256
KINDS = ("two", "dir", "acc", "own")
FIRST = 1
USES = {
    "two": ((2, 0), (2, 1)), "dir": ((1, 1), (3, 0)),
    "acc": ((1, 0), (3, 1)), "own": ((0, 0), (0, 1)),
}
STEPS = {"two": 2, "dir": 2, "acc": 2, "own": 1}
TURN = {"dir": 0, "two": 1, "acc": 2, "own": 3}


class Item:
    def __init__(self, key, deps, rank, emit, link=None, size=0, takes=0.0, late=0.0):
        self.key, self.deps, self.rank, self.emit = key, deps, rank, emit
        self.link, self.size, self.takes, self.late = link, size, takes, late


def plan(items):
    ready, free, order = {}, {}, []
    left = list(items)
    now = 0.0
    while left:
        best = None
        able = [
            (item, max([ready[d] for d in item.deps], default=0.0))
            for item in left if all(d in ready for d in item.deps)
        ]
        for item, at in able:
            if item.link:
                at = max(at, free.get(item.link, 0.0) - WINDOW, now)
                until = max(free.get(item.link, 0.0), at) + SLACK
                for other, when in able:
                    sooner = other.link == item.link and other.rank[0] < item.rank[0] - 1
                    if sooner and at < when <= until:
                        at = when + 0.01
            trial = (max(at, now), 0 if item.link else 1, item.rank)
            if best is None or trial < best[0]:
                best = (trial, item)
        (now, _, _), item = best
        if item.link:
            near = item.link == "core"
            begin = max(now, free.get(item.link, 0.0))
            free[item.link] = begin + item.size / (CORE_RATE if near else LINK_RATE)
            ready[item.key] = free[item.link] + (CORE_LATENCY if near else LINK_LATENCY) + item.late
            now += 0.03
        else:
            now += item.takes
            ready[item.key] = now
        order.append(item)
        left.remove(item)
    return order, ready


def kernel(xs, ys, zs, a_hbm, b_hbm, out, left, right, relay, sums_own, *rest):
    parts = len(GROUPS)
    code_out, rest = rest[:parts], rest[parts:]
    code_in, rest = rest[:parts], rest[parts:]
    (peak, gain_out), rest = rest[:2], rest[2:]
    sums_in, rest = rest[:2], rest[2:]
    load, a_sent, b_sent, c_sent, s_sent, came, a_came, b_came, two_came, end_came, s_came = rest
    rows, depth = a_hbm.shape
    columns = b_hbm.shape[1]
    n = ys * zs
    half = columns // 2
    start = [sum(GROUPS[:p]) for p in range(parts)]
    inner = depth * zs

    me_north, me = lax.axis_index("north"), lax.axis_index("east")
    x, core = lax.div(me_north, 2), lax.rem(me_north, 2)
    z, y = lax.div(me, ys), lax.rem(me, ys)

    def turn(v, by, size):
        return lax.rem(v + (by + size), size)

    def x_at(by):
        return 2 * turn(x, by, xs) + core

    def y_at(by):
        return z * ys + turn(y, by, ys)

    def z_at(by):
        return turn(z, by, zs) * ys + y

    partner = (2 * x + 1 - core, me)
    toward = {
        "x0": (x_at(1), me), "x1": (x_at(-1), me),
        "y0": (me_north, y_at(1)), "y1": (me_north, y_at(-1)),
        "z0": (me_north, z_at(1)), "z1": (me_north, z_at(-1)),
        "core": partner,
    }

    def slab(north):
        return pl.ds(pl.multiple_of(north * depth, depth), depth)

    def width(kind):
        return half // STEPS[kind]

    def cols(kind, d, b):
        return pl.ds(USES[kind][d][1] * half + b * width(kind), width(kind))

    def right_piece(kind, d, b, north):
        return right.at[
            KINDS.index(kind), slab(north), pl.ds((2 * b + d) * width(kind), width(kind))
        ]

    load_a = pltpu.make_async_copy(a_hbm, left.at[pl.ds(HEAD, rows), slab(z)], load.at[0])
    load_b = pltpu.make_async_copy(
        b_hbm.at[slab(y)], right.at[KINDS.index("own"), slab(me_north)], load.at[1]
    )
    load_a.start()
    load_b.start()

    barrier = pltpu.get_barrier_semaphore()
    for device in toward.values():
        pl.semaphore_signal(barrier, inc=1, device_id=device, device_id_type=MESH)
    load_a.wait()
    largest = jnp.max(jnp.abs(left[pl.ds(HEAD, rows), slab(z)].astype(jnp.float32)), axis=0, keepdims=True)
    largest = jnp.broadcast_to(jnp.max(largest, axis=1, keepdims=True), (HEAD, depth))
    left[pl.ds(0, HEAD), slab(z)] = largest.astype(left.dtype)
    pl.semaphore_wait(barrier, len(toward))

    def whole(ref, sem):
        return pltpu.make_async_remote_copy(
            src_ref=ref, dst_ref=ref, send_sem=sem, recv_sem=sem,
            device_id=partner, device_id_type=MESH,
        )

    items = []
    waits = {("load", 1): load_b.wait}
    for key in list(waits):
        items.append(Item(key, [], (-1.0,), lambda: None))
    single = []

    def send(key, deps, rank, link, source, target, sent, arrives=None, late=0.0):
        if arrives is None:
            arrives = came.at[len(single)]
            single.append(key)
        copy = pltpu.make_async_remote_copy(
            src_ref=source, dst_ref=target, send_sem=sent, recv_sem=arrives,
            device_id=toward[link], device_id_type=MESH,
        )
        if single and single[-1] == key:
            waits[key] = copy.wait_recv
        size = 2 * source.shape[0] * source.shape[1]
        items.append(Item(key, deps, (rank,), copy.start, link, size, late=late))

    arrived = []
    for p in range(parts):
        chunk = GROUPS[p] // 2
        last = []
        for s in range(2):
            head = HEAD if p + s == 0 else 0
            here = pl.ds(HEAD - head + start[p] + s * chunk, head + chunk)
            source = pl.ds(start[p] + s * chunk, chunk)
            for d in range(2):
                hops = zs // 2 - (s + d) % 2
                for h in range(hops):
                    block = left.at[here, slab(turn(z, h if d else -h, zs))]
                    key = ("a", p, s, d, h)
                    send(
                        key, [("a", p, s, d, h - 1)] if h else [], PACE * min(p, parts - 2) + h + 0.01 * s, f"z{d}",
                        block if h or head else a_hbm.at[source], block, a_sent.at[0],
                        a_came.at[p] if h == hops - 1 else None, 0 if h else FAR_SOURCE,
                    )
                last.append(key)
        key = ("a", p)
        items.append(Item(key, last, (-1.0,), lambda: None))
        size = left.at[pl.ds(0, 4 * chunk + (0 if p else 2 * HEAD)), pl.ds(0, depth)]
        waits[key] = whole(size, a_came.at[p]).wait_recv
        arrived.append([key])

    have = {}
    for i, kind in enumerate(KINDS):
        for b in range(STEPS[kind]):
            rank = 3 * TURN[kind] + 1.5 * b
            have[kind, b] = [("b", kind, b)] + ([("load", 1)] if kind == "own" else [])
            near = []
            for d, (j, h) in enumerate(USES[kind]):
                u = (kind, d, b)
                mine = right_piece(*u, me_north)
                base = [("by", u)] if j else []
                if j:
                    target = b_hbm.at[slab(turn(y, -j, ys)), cols(*u)]
                    link = f"y{h}" if j == 2 else ("y0" if j == 3 else "y1")
                    if j == 2:
                        send(
                            ("far", u), [], rank, link, target, relay.at[h, b], b_sent.at[0],
                            late=FAR_SOURCE,
                        )
                        send(("by", u), [("far", u)], rank, link, relay.at[h, b], mine, b_sent.at[0])
                    else:
                        send(("by", u), [], rank, link, target, mine, b_sent.at[0], late=FAR_SOURCE)
                source = mine if j else b_hbm.at[slab(y), cols(*u)]
                for e in range(2):
                    send(
                        ("bx", u, e, 1), base, rank + (0.0 if e == h else 0.1), f"x{e}",
                        source, mine, b_sent.at[0], late=0 if j else FAR_SOURCE,
                    )
                passed = right_piece(*u, x_at(1 if h else -1))
                send(
                    ("bx", u, h, 2), [("bx", u, h, 1)], rank - 1, f"x{h}",
                    passed, passed, b_sent.at[0],
                )
                have[kind, b] += base + [("bx", u, 0, 1), ("bx", u, 1, 1), ("bx", u, h, 2)]
                for t in range(xs):
                    place = right_piece(*u, x_at(-t))
                    deps = [base, [("bx", u, 0, 1)], [("bx", u, h, 2)], [("bx", u, 1, 1)]][t]
                    send(
                        ("bd", u, t), deps, rank, "core", place if t else source, place,
                        b_sent.at[0], b_came.at[2 * i + b],
                    )
                    near.append(("bd", u, t))
            items.append(Item(("b", kind, b), near, (-1.0,), lambda: None))
            size = right.at[i, pl.ds(0, depth * xs), pl.ds(0, 2 * width(kind))]
            waits["b", kind, b] = whole(size, b_came.at[2 * i + b]).wait_recv

    def multiply(p, kind, b=None):
        across = slice(None) if b is None else slice(b * half, (b + 1) * half)
        return jnp.dot(
            left[HEAD + start[p]:HEAD + start[p] + GROUPS[p], :], right[KINDS.index(kind), :, across],
            preferred_element_type=jnp.float32,
        )

    def scale_in(k, across):
        return code_in[0][k, GROUPS[0]:GROUPS[0] + 1, across].astype(jnp.float32)

    def decode(p, k, across):
        coded = code_in[p][k, :GROUPS[p], across].astype(jnp.float32)
        size = lax.rsqrt(lax.rsqrt(jnp.maximum(jnp.abs(coded), 1e-37)))
        size = size * lax.rsqrt(size)
        return jnp.where(coded < 0, -size, size) * (scale_in(k, across) * (1.0 / TOP))

    def encode(p, k, across, value):
        power = value * gain_out[k, :, across]
        power = power * power
        power = power * power
        power = power * power
        code_out[p][k, :GROUPS[p], across] = jnp.where(value < 0, -power, power).astype(jnp.bfloat16)

    def set_scale(kind, b):
        i = KINDS.index(kind)
        if kind == KINDS[FIRST]:
            if b == 0:
                most = jnp.max(left[:HEAD, :].astype(jnp.float32), axis=0, keepdims=True)
                peak[...] = jnp.broadcast_to(jnp.max(most, axis=1, keepdims=True) * inner, peak.shape)
        for d in range(2):
            first = (2 * b + d) * width(kind)
            across = slice(b * width(kind), (b + 1) * width(kind))
            block = right[i, :, first:first + width(kind)]
            bound = jnp.max(jnp.abs(block.astype(jnp.float32)), axis=0, keepdims=True) * peak[...]
            if kind == "acc":
                bound = bound + scale_in(slot("two", d), across)
            scale = jnp.maximum(bound, 1e-30).astype(jnp.bfloat16)
            gain_out[slot(kind, d), :, across] = TOP / scale.astype(jnp.float32)
            code_out[0][slot(kind, d), GROUPS[0]:, across] = jnp.broadcast_to(scale, (TAIL, width(kind)))

    def slot(kind, d):
        return 2 * KINDS.index(kind) + d

    def part(p, kind, b):
        def run():
            if p == 0:
                set_scale(kind, b)
            value = multiply(p, kind, b)
            for c in range(STEPS[kind]) if b is None else (b,):
                across = slice(c * width(kind), (c + 1) * width(kind))
                for d in range(2):
                    first = (2 * (c if b is None else 0) + d) * width(kind)
                    block = value[:, first:first + width(kind)]
                    if kind == "acc":
                        block = block + decode(p, slot("two", d), across)
                    encode(p, slot(kind, d), across, block)
        return run

    def own(p):
        def run():
            out[start[p]:start[p] + GROUPS[p], :] = multiply(p, "own")
        return run

    def finish(p):
        def run():
            here = slice(start[p], start[p] + GROUPS[p])
            narrow = None
            for h in range(2):
                value = out[here, h * half:(h + 1) * half]
                value = value + decode(p, slot("dir", 1 - h), slice(None)) + decode(p, slot("acc", h), slice(None))
                out[here, h * half:(h + 1) * half] = value
                value = value * value
                for k in range(0, half, LANES):
                    term = value[:, k:k + LANES]
                    narrow = term if narrow is None else narrow + term
            sums_own[:, here] = jnp.sum(narrow.T, axis=0, keepdims=True)
        return run

    for p in range(parts):
        sent_rows = pl.ds(0, GROUPS[p] + (0 if p else TAIL))
        ends = []
        for k, kind in enumerate(KINDS[:3]):
            split = STEPS[kind] == 2 and p < EARLY
            for b in range(2) if split else (None,):
                deps = list(arrived[p])
                for c in range(STEPS[kind]) if b is None else (b,):
                    deps += have[kind, c]
                c = b or 0
                if kind == "acc":
                    deps.append(("two", p, c))
                if p:
                    deps += [("k", 0, kind, e) for e in range(2)]
                if kind != KINDS[FIRST]:
                    deps.append(("k", 0, KINDS[FIRST], 0))
                rank = 3 * p + 4 * k + 0.1 * c
                takes = (MULTIPLY * (0.95 if split else 1.0) + CODE * (0.5 if split else 1.0)) * GROUPS[p] + (0 if p else 0.2)
                items.append(Item(("k", p, kind, c), deps, (rank,), part(p, kind, b), takes=takes))
                across = pl.ds(c * half // 2, half // 2) if split else pl.ds(0, half)
                for d in range(2):
                    i = slot(kind, d)
                    send(
                        ("c", p, kind, c, d), [("k", p, kind, c)], rank, f"y{d}",
                        code_out[p].at[i, sent_rows, across], code_in[p].at[i, sent_rows, across], c_sent.at[p],
                        two_came.at[2 * p + c] if kind == "two" else end_came.at[p],
                    )
                sent = [("c", p, kind, c, d) for d in range(2)]
                if kind == "two":
                    items.append(Item(("two", p, c), sent, (-1.0,), lambda: None))
                    size = code_in[p].at[pl.ds(0, 2), sent_rows, across]
                    waits["two", p, c] = whole(size, two_came.at[2 * p + c]).wait_recv
                else:
                    ends += sent
        deps = arrived[p] + have["own", 0]
        items.append(Item(("own", p), deps, (1000 + p,), own(p), takes=MULTIPLY * GROUPS[p]))
        items.append(Item(("end", p), ends, (-1.0,), lambda: None))
        waits["end", p] = whole(code_in[p].at[pl.ds(2, 4), sent_rows], end_came.at[p]).wait_recv
        deps = [("own", p), ("end", p), ("end", 0)]
        items.append(Item(("fin", p), deps, (500 + p,), finish(p), takes=FINISH * GROUPS[p]))

    shares = ((0, start[LATE]), (start[LATE], rows - start[LATE]))

    def tell(i):
        def run():
            for k in range(1, n):
                pltpu.make_async_remote_copy(
                    src_ref=sums_own.at[:, pl.ds(*shares[i])], dst_ref=sums_in[i].at[k - 1],
                    send_sem=s_sent.at[i], recv_sem=s_came.at[i],
                    device_id=(me_north, lax.rem(me + k, n)), device_id_type=MESH,
                ).start()
        return run

    early = [("fin", p) for p in range(LATE)]
    items.append(Item(("s", 0), early, (2000,), tell(0), takes=0.3))
    late = [("fin", p) for p in range(LATE, parts)]
    items.append(Item(("s", 1), late + [("s", 0)], (2001,), tell(1), takes=0.3))

    order, _ = plan(items)
    waited = set()
    for item in order:
        for key in item.deps:
            if key in waits and key not in waited:
                waits[key]()
                waited.add(key)
        item.emit()

    piece = 128
    for i, (begin, count) in enumerate(shares):
        whole(sums_in[i], s_came.at[i]).wait_recv()
        total = sums_own[:, pl.ds(begin, count)]
        for k in range(n - 1):
            total = total + sums_in[i][k]
        scale = lax.rsqrt(total / (columns * n) + 1e-06)
        for r in range(0, count, piece):
            gain = jnp.broadcast_to(scale[:, r:r + piece], (LANES, piece)).T
            for k in range(0, columns, LANES):
                out[pl.ds(begin + r, piece), k:k + LANES] *= gain
    whole(left.at[:, pl.ds(0, depth * (zs - 1))], a_sent.at[0]).wait_send()
    whole(right, b_sent.at[0]).wait_send()
    for p in range(parts):
        whole(code_out[p], c_sent.at[p]).wait_send()
    for i in range(2):
        whole(sums_in[i], s_sent.at[i]).wait_send()


def shards(xs, ys, zs, left, right):
    rows, depth = left.shape
    columns = right.shape[1]
    half = columns // 2
    parts = len(GROUPS)
    peers = ys * zs - 1
    dma = pltpu.SemaphoreType.DMA
    codes = [pltpu.VMEM((6, group + (0 if p else TAIL), half), jnp.bfloat16) for p, group in enumerate(GROUPS)]
    pieces = sum(2 * STEPS[kind] for kind in KINDS)
    single = parts * (2 * (zs - 1) - 4) + 3 * pieces + sum(2 * STEPS[kind] for kind in KINDS[:3]) + 2 * STEPS["two"]
    factors = [pltpu.with_memory_space_constraint(v, pltpu.HBM) for v in (left, right)]
    return pl.pallas_call(
        functools.partial(kernel, xs, ys, zs),
        out_shape=jax.ShapeDtypeStruct((rows, columns), jnp.float32),
        in_specs=[pl.BlockSpec(memory_space=pltpu.HBM)] * 2,
        out_specs=pl.BlockSpec(memory_space=pltpu.VMEM),
        scratch_shapes=[
            pltpu.VMEM((HEAD + rows, depth * zs), left.dtype),
            pltpu.VMEM((len(KINDS), depth * 2 * xs, columns), right.dtype),
            pltpu.VMEM((2, STEPS["two"], depth, half // STEPS["two"]), right.dtype),
            pltpu.VMEM((1, rows), jnp.float32),
            *codes,
            *codes,
            pltpu.VMEM((1, half // 2), jnp.float32),
            pltpu.VMEM((6, 1, half), jnp.float32),
            pltpu.VMEM((peers, 1, sum(GROUPS[:LATE])), jnp.float32),
            pltpu.VMEM((peers, 1, sum(GROUPS[LATE:])), jnp.float32),
            dma((2,)),
            dma((1,)),
            dma((1,)),
            dma((parts,)),
            dma((2,)),
            dma((single,)),
            dma((parts,)),
            dma((2 * len(KINDS),)),
            dma((2 * parts,)),
            dma((parts,)),
            dma((2,)),
        ],
        compiler_params=pltpu.CompilerParams(
            collective_id=0, has_side_effects=True, vmem_limit_bytes=40 << 20
        ),
    )(*factors)


def solution(mesh):
    xs = mesh.shape["north"] // 2
    ys = xs
    zs = mesh.shape["east"] // ys
    placed = (P("north", "east"), P("north", "east"))
    return jax.shard_map(
        functools.partial(shards, xs, ys, zs),
        mesh=mesh, in_specs=placed, out_specs=P("north", "east"), check_vma=False,
    )
```

time: 93.2 us -> 77.8 us (0.83)
  Pallas kernels: 90 us -> 76.4 us
  local copies, waits for them, and re-layouts: 3.08 us -> 1.32 us
    pallas_call x1, Pallas kernels: 90 us -> 76.4 us  [shards(): pl.pallas_call(functools.partial(kernel, xs, ys, zs), out_shape=jax.Shape...]
    unnamed x1, local copies, waits for them, and re-layouts: 3.08 us -> 1.32 us
where the time goes in v1:
time: 77.8 us; the launch traced here: 77.7 us
  Pallas kernels  76.4 us (98%)
  local copies, waits for them, and re-layouts  1.32 us (2%)
    pallas_call x1, Pallas kernels, shards(): pl.pallas_call(functools.partial(kernel, xs, ys, zs), out_shape=jax.Shape...  76.4 us

profile of v1, /device:TPU:1, one launch (start us, length us, event | category | flops | bytes accessed | tf_op | source)
XLA Modules:
  0.0 77.7 jit_solution(1980678660602683704)
XLA Ops:
  0.0 76.4 %shard_map.28 = f32[1024,512]{1,0:T(8,128)S(1)} custom-call(bf16[1024,256]{1,0:T(8,128)(2,1)} %a_hbm.1, bf16[1024,512]{1,0:T(8,128)(2,1)} %b_hbm.1), custom_call_target="tpu_custom_call" | custom-call | tf_op jit(solution)/shard_map/pallas_call | solution.py:419
  76.4 1.3 %copy.4 = f32[1024,512]{1,0:T(8,128)} copy(f32[1024,512]{1,0:T(8,128)S(1)} %shard_map.28) | data formatting | bytes 4194304

commit v2 on v1

--- a/solution.py
+++ b/solution.py
@@ -15,12 +15,12 @@
 TOP = 32768.0
 TAIL = 8
 HEAD = 16
-LINK_RATE = 46.6e3
+LINK_RATE = 45e3
 CORE_RATE = 600e3
 LINK_LATENCY = 2.8
 CORE_LATENCY = 1.0
 FAR_SOURCE = 0.5
-WINDOW = 2.5
+WINDOW = 3.5
 SLACK = 0.0
 PACE = 3
 MULTIPLY = 0.7 / 256
@@ -140,11 +140,13 @@
     barrier = pltpu.get_barrier_semaphore()
     for device in toward.values():
         pl.semaphore_signal(barrier, inc=1, device_id=device, device_id_type=MESH)
-    load_a.wait()
-    largest = jnp.max(jnp.abs(left[pl.ds(HEAD, rows), slab(z)].astype(jnp.float32)), axis=0, keepdims=True)
-    largest = jnp.broadcast_to(jnp.max(largest, axis=1, keepdims=True), (HEAD, depth))
-    left[pl.ds(0, HEAD), slab(z)] = largest.astype(left.dtype)
     pl.semaphore_wait(barrier, len(toward))
+
+    def set_head():
+        part = left[pl.ds(HEAD, rows), slab(z)].astype(jnp.float32)
+        most = jnp.max(jnp.abs(part), axis=0, keepdims=True)
+        most = jnp.broadcast_to(jnp.max(most, axis=1, keepdims=True), (HEAD, depth))
+        left[pl.ds(0, HEAD), slab(z)] = most.astype(left.dtype)
 
     def whole(ref, sem):
         return pltpu.make_async_remote_copy(
@@ -153,9 +155,10 @@
         )
 
     items = []
-    waits = {("load", 1): load_b.wait}
+    waits = {("load", 0): load_a.wait, ("load", 1): load_b.wait}
     for key in list(waits):
         items.append(Item(key, [], (-1.0,), lambda: None))
+    items.append(Item(("head",), [("load", 0)], (-0.5,), set_head, takes=0.3))
     single = []
 
     def send(key, deps, rank, link, source, target, sent, arrives=None, late=0.0):
@@ -176,16 +179,17 @@
         chunk = GROUPS[p] // 2
         last = []
         for s in range(2):
-            head = HEAD if p + s == 0 else 0
-            here = pl.ds(HEAD - head + start[p] + s * chunk, head + chunk)
-            source = pl.ds(start[p] + s * chunk, chunk)
+            head = HEAD if p == 0 and s == 1 else 0
+            begin = start[p] + (s if p else 1 - s) * chunk
+            here = pl.ds(HEAD - head + begin, head + chunk)
+            source = pl.ds(begin, chunk)
             for d in range(2):
                 hops = zs // 2 - (s + d) % 2
                 for h in range(hops):
                     block = left.at[here, slab(turn(z, h if d else -h, zs))]
                     key = ("a", p, s, d, h)
                     send(
-                        key, [("a", p, s, d, h - 1)] if h else [], PACE * min(p, parts - 2) + h + 0.01 * s, f"z{d}",
+                        key, [("a", p, s, d, h - 1)] if h else [("head",)] if head else [], PACE * min(p, parts - 2) + h + 0.01 * s, f"z{d}",
                         block if h or head else a_hbm.at[source], block, a_sent.at[0],
                         a_came.at[p] if h == hops - 1 else None, 0 if h else FAR_SOURCE,
                     )

time: 77.8 us -> 76.4 us (0.982)
  Pallas kernels: 76.4 us -> 75 us
    pallas_call x1, Pallas kernels: 76.4 us -> 75 us  [shards(): pl.pallas_call(functools.partial(kernel, xs, ys, zs), out_shape=jax.Shape...]
where the time goes in v2:
time: 76.4 us; the launch traced here: 76.3 us
  Pallas kernels  75 us (98%)
  local copies, waits for them, and re-layouts  1.32 us (2%)
    pallas_call x1, Pallas kernels, shards(): pl.pallas_call(functools.partial(kernel, xs, ys, zs), out_shape=jax.Shape...  75 us

profile of v2, /device:TPU:1, one launch (start us, length us, event | category | flops | bytes accessed | tf_op | source)
XLA Modules:
  0.0 76.3 jit_solution(11582120881070460661)
XLA Ops:
  0.0 75.0 %shard_map.28 = f32[1024,512]{1,0:T(8,128)S(1)} custom-call(bf16[1024,256]{1,0:T(8,128)(2,1)} %a_hbm.1, bf16[1024,512]{1,0:T(8,128)(2,1)} %b_hbm.1), custom_call_target="tpu_custom_call" | custom-call | tf_op jit(solution)/shard_map/pallas_call | solution.py:423
  75.0 1.3 %copy.4 = f32[1024,512]{1,0:T(8,128)} copy(f32[1024,512]{1,0:T(8,128)S(1)} %shard_map.28) | data formatting | bytes 4194304

commit v3 on v2

--- a/solution.py
+++ b/solution.py
@@ -323,6 +323,9 @@
             sums_own[:, here] = jnp.sum(narrow.T, axis=0, keepdims=True)
         return run
 
+    def turn_of(p, c):
+        return 2 * p + c if p < EARLY else EARLY + p
+
     for p in range(parts):
         sent_rows = pl.ds(0, GROUPS[p] + (0 if p else TAIL))
         ends = []
@@ -348,13 +351,13 @@
                     send(
                         ("c", p, kind, c, d), [("k", p, kind, c)], rank, f"y{d}",
                         code_out[p].at[i, sent_rows, across], code_in[p].at[i, sent_rows, across], c_sent.at[p],
-                        two_came.at[2 * p + c] if kind == "two" else end_came.at[p],
+                        two_came.at[turn_of(p, c)] if kind == "two" else end_came.at[p],
                     )
                 sent = [("c", p, kind, c, d) for d in range(2)]
                 if kind == "two":
                     items.append(Item(("two", p, c), sent, (-1.0,), lambda: None))
                     size = code_in[p].at[pl.ds(0, 2), sent_rows, across]
-                    waits["two", p, c] = whole(size, two_came.at[2 * p + c]).wait_recv
+                    waits["two", p, c] = whole(size, two_came.at[turn_of(p, c)]).wait_recv
                 else:
                     ends += sent
         deps = arrived[p] + have["own", 0]
@@ -366,9 +369,11 @@
 
     shares = ((0, start[LATE]), (start[LATE], rows - start[LATE]))
 
+    farthest = sorted(range(1, n), key=lambda k: abs(k - n // 2))
+
     def tell(i):
         def run():
-            for k in range(1, n):
+            for k in farthest:
                 pltpu.make_async_remote_copy(
                     src_ref=sums_own.at[:, pl.ds(*shares[i])], dst_ref=sums_in[i].at[k - 1],
                     send_sem=s_sent.at[i], recv_sem=s_came.at[i],
@@ -443,8 +448,8 @@
             dma((2,)),
             dma((single,)),
             dma((parts,)),
-            dma((2 * len(KINDS),)),
-            dma((2 * parts,)),
+            dma((2 * len(KINDS) - 1,)),
+            dma((EARLY + parts,)),
             dma((parts,)),
             dma((2,)),
         ],

time: 76.4 us -> 76.2 us (level)
  no operation moved by 1% of the time
where the time goes in v3:
time: 76.2 us; the launch traced here: 76.1 us
  Pallas kernels  74.8 us (98%)
  local copies, waits for them, and re-layouts  1.32 us (2%)
    pallas_call x1, Pallas kernels, shards(): pl.pallas_call(functools.partial(kernel, xs, ys, zs), out_shape=jax.Shape...  74.8 us

profile of v3, /device:TPU:1, one launch (start us, length us, event | category | flops | bytes accessed | tf_op | source)
XLA Modules:
  0.0 76.1 jit_solution(3197267270706933057)
XLA Ops:
  0.0 74.8 %shard_map.28 = f32[1024,512]{1,0:T(8,128)S(1)} custom-call(bf16[1024,256]{1,0:T(8,128)(2,1)} %a_hbm.1, bf16[1024,512]{1,0:T(8,128)(2,1)} %b_hbm.1), custom_call_target="tpu_custom_call" | custom-call | tf_op jit(solution)/shard_map/pallas_call | solution.py:428
  74.8 1.3 %copy.4 = f32[1024,512]{1,0:T(8,128)} copy(f32[1024,512]{1,0:T(8,128)S(1)} %shard_map.28) | data formatting | bytes 4194304

commit v4 on v3

--- a/solution.py
+++ b/solution.py
@@ -20,7 +20,7 @@
 LINK_LATENCY = 2.8
 CORE_LATENCY = 1.0
 FAR_SOURCE = 0.5
-WINDOW = 3.5
+WINDOW = 3.8
 SLACK = 0.0
 PACE = 3
 MULTIPLY = 0.7 / 256

time: 76.2 us -> 77.5 us (1.017)
  Pallas kernels: 74.8 us -> 76.1 us
    pallas_call x1, Pallas kernels: 74.8 us -> 76.1 us  [shards(): pl.pallas_call(functools.partial(kernel, xs, ys, zs), out_shape=jax.Shape...]
where the time goes in v4:
time: 77.5 us; the launch traced here: 77.4 us
  Pallas kernels  76.1 us (98%)
  local copies, waits for them, and re-layouts  1.32 us (2%)
    pallas_call x1, Pallas kernels, shards(): pl.pallas_call(functools.partial(kernel, xs, ys, zs), out_shape=jax.Shape...  76.1 us

profile of v4, /device:TPU:1, one launch (start us, length us, event | category | flops | bytes accessed | tf_op | source)
XLA Modules:
  0.0 77.4 jit_solution(9949431216819211944)
XLA Ops:
  0.0 76.1 %shard_map.28 = f32[1024,512]{1,0:T(8,128)S(1)} custom-call(bf16[1024,256]{1,0:T(8,128)(2,1)} %a_hbm.1, bf16[1024,512]{1,0:T(8,128)(2,1)} %b_hbm.1), custom_call_target="tpu_custom_call" | custom-call | tf_op jit(solution)/shard_map/pallas_call | solution.py:428
  76.1 1.3 %copy.4 = f32[1024,512]{1,0:T(8,128)} copy(f32[1024,512]{1,0:T(8,128)S(1)} %shard_map.28) | data formatting | bytes 4194304
